TPU v7x, 64 devices: a 2x2x8 block of a 4x4x8 slice. The times are simulated.
64 devices in a mesh: dp: 4 (over x, y), tp: 16 (over z, core).
Axes of the slice: x: 2, y: 2, z: 8, core: 2. Of those that a mesh axis runs over, the one named last changes fastest.
The devices are a block of a 4x4x8 slice.
Arguments:
- x_norm: bfloat16 [32768, 2048], P(('dp', 'tp')), parts along dimension 0
- grad_out: bfloat16 [32768, 2048], P(('dp', 'tp')), parts along dimension 0
- w_gate: bfloat16 [2048, 5632], P(None, 'tp')
- w_up: bfloat16 [2048, 5632], P(None, 'tp')
- w_down: bfloat16 [5632, 2048], P('tp')
Outputs:
- output 1: bfloat16 [32768, 2048], P(('dp', 'tp')), parts along dimension 0
- output 2: float32 [8192, 5632], P('dp', 'tp'), parts along dimension 0
- output 3: float32 [8192, 5632], P('dp', 'tp'), parts along dimension 0
- output 4: float32 [22528, 2048], P(('dp', 'tp')), parts along dimension 0
There are 4 independent parts. A program takes and returns all parts, laid end to end along the dimension named above; an argument that names none is the same for every part.
All inputs are finite; a program needn't handle non-finite values.
Results may differ from a plain program's by a relative error of at most 0.0166201.
Values are sent between devices in bfloat16 or wider.
A program may use at most 768 MiB of HBM per device.

v0:
```python
import jax
import jax.numpy as jnp
from jax import lax
from jax.sharding import PartitionSpec as P


def solution(mesh):
    contract_rows = (((0,), (0,)), ((), ()))
    contract_cols = (((1,), (1,)), ((), ()))

    def device_step(x_shard, dy_shard, w_gate, w_up, w_down):
        x_all = lax.all_gather(x_shard, "tp", axis=0, tiled=True)
        gate_pre = jnp.dot(x_all, w_gate, preferred_element_type=jnp.float32).astype(jnp.bfloat16)
        up_pre = jnp.dot(x_all, w_up, preferred_element_type=jnp.float32).astype(jnp.bfloat16)
        dy_all = lax.all_gather(dy_shard, "tp", axis=0, tiled=True)
        gate_f = gate_pre.astype(jnp.float32)
        up_f = up_pre.astype(jnp.float32)
        gate_sig = jax.nn.sigmoid(gate_f)
        gate_act = gate_f * gate_sig
        mid_act = (gate_act * up_f).astype(jnp.bfloat16)
        grad_w_down = lax.dot_general(mid_act, dy_all, contract_rows, preferred_element_type=jnp.float32)
        grad_mid = lax.dot_general(dy_all, w_down, contract_cols, preferred_element_type=jnp.float32)
        grad_up = (grad_mid * gate_act).astype(jnp.bfloat16)
        grad_gate = (grad_mid * up_f * gate_sig * (1.0 + gate_f * (1.0 - gate_sig))).astype(jnp.bfloat16)
        partial_x = (lax.dot_general(grad_gate, w_gate, contract_cols, preferred_element_type=jnp.float32)
                     + lax.dot_general(grad_up, w_up, contract_cols, preferred_element_type=jnp.float32))
        grad_x = lax.psum_scatter(partial_x.astype(jnp.bfloat16), "tp", scatter_dimension=0, tiled=True)
        grad_w_gate = lax.dot_general(x_all, grad_gate, contract_rows, preferred_element_type=jnp.float32)
        grad_w_up = lax.dot_general(x_all, grad_up, contract_rows, preferred_element_type=jnp.float32)
        return grad_x, grad_w_gate, grad_w_up, grad_w_down

    tok_spec = P(("dp", "tp"), None)
    col_spec = P(None, "tp")
    grad_col_spec = P("dp", "tp")
    return jax.shard_map(device_step, mesh=mesh,
                         in_specs=(tok_spec, tok_spec, col_spec, col_spec, P("tp", None)),
                         out_specs=(tok_spec, grad_col_spec, grad_col_spec, tok_spec),
                         check_vma=False)
```

profile of v0, /device:TPU:21, one launch (start us, length us, event | category | flops | bytes accessed | tf_op | source)
XLA Modules:
  0.0 646.2 jit_solution(15769005748078948833)
XLA Ops:
  7.2 0.0 copy-start
  7.2 0.1 all-gather.5.cloned.1.call-start
  7.3 0.7 all-gather.5.cloned.1.call-update
  8.0 0.1 all-gather.3.cloned.1.call-start
  8.1 0.7 all-gather.3.cloned.1.call-update
  8.8 0.0 copy-start.2
  8.8 0.1 reduce-scatter.2.cloned.1.call-start
  8.9 176.9 %all-gather.5.cloned.1.call-done = bf16[8192,2048]{1,0:T(8,128)(2,1)} async-done(((bf16[512,2048]{1,0:T(8,128)(2,1)}), bf16[8192,2048]{1,0:T(8,128)(2,1)}) %all-gather.5.cloned.1.call-update) | async-done | bytes 33554448 | tf_op jit(solution)/shard_map/all_gather | solution.py:12
  185.7 0.0 copy-done
  185.7 19.7 %convolution_convert_fusion = bf16[8192,352]{0,1:T(8,128)(2,1)} fusion(bf16[8192,2048]{1,0:T(8,128)(2,1)} %all-gather.5.cloned.1.call-done, bf16[2048,352]{0,1:T(8,128)(2,1)S(1)} %copy-done), kind=kOutput, calls=%fused_computation.15 | convolution fusion | flops 11814043648 | bytes 40763392 | tf_op jit(solution)/shard_map/dot_general | solution.py:13
  205.4 0.0 copy-done.2
  205.4 19.7 %convolution_convert_fusion.1 = bf16[8192,352]{0,1:T(8,128)(2,1)} fusion(bf16[8192,2048]{1,0:T(8,128)(2,1)} %all-gather.5.cloned.1.call-done, bf16[2048,352]{0,1:T(8,128)(2,1)S(1)} %copy-done.2), kind=kOutput, calls=%fused_computation.16 | convolution fusion | flops 11814043648 | bytes 40763392 | tf_op jit(solution)/shard_map/dot_general | solution.py:14
  225.1 131.9 %all-gather.3.cloned.1.call-done = bf16[8192,2048]{1,0:T(8,128)(2,1)} async-done(((bf16[512,2048]{1,0:T(8,128)(2,1)}), bf16[8192,2048]{1,0:T(8,128)(2,1)}) %all-gather.3.cloned.1.call-update) | async-done | bytes 33554448 | tf_op jit(solution)/shard_map/all_gather | solution.py:15
  357.0 28.3 %fusion.2 = (bf16[8192,352]{0,1:T(8,128)(2,1)}, f32[8192,352]{0,1:T(8,128)}) fusion(bf16[8192,352]{0,1:T(8,128)(2,1)} %convolution_convert_fusion.1, bf16[8192,352]{0,1:T(8,128)(2,1)} %convolution_convert_fusion, bf16[8192,2048]{1,0:T(8,128)(2,1)} %all-gather.3.cloned.1.call-done, bf16[352,2048]{1,0:T(8,128)(2,1)} %param.9), kind=kOutput, calls=%fused_computation.8 | convolution fusion | flops 11845763072 | bytes 63832064 | tf_op jit(solution)/shard_map/dot_general | solution.py:22
  385.2 28.3 %fusion.11 = f32[8192,2048]{1,0:T(8,128)} fusion(bf16[8192,352]{0,1:T(8,128)(2,1)} %get-tuple-element.4, bf16[2048,352]{0,1:T(8,128)(2,1)S(1)} %copy-done), kind=kOutput, calls=%fused_computation.21 | convolution fusion | flops 11811160064 | bytes 74317824 | tf_op jit(solution)/shard_map/dot_general | solution.py:25
  413.5 46.4 %add_convert_fusion = bf16[8192,2048]{1,0:T(8,128)(2,1)} fusion(f32[8192,2048]{1,0:T(8,128)} %fusion.11, bf16[2048,352]{0,1:T(8,128)(2,1)S(1)} %copy-done.2, f32[8192,352]{0,1:T(8,128)} %get-tuple-element.5, bf16[8192,352]{0,1:T(8,128)(2,1)} %convolution_convert_fusion), kind=kOutput, calls=%fused_computation | convolution fusion | flops 11864899584 | bytes 119406592 | tf_op jit(solution)/shard_map/dot_general | solution.py:26
  459.9 0.1 reduce-scatter.2.cloned.1.call-update
  460.0 20.7 %convolution_bitcast_fusion.1 = f32[2048,352]{0,1:T(8,128)} fusion(bf16[8192,352]{0,1:T(8,128)(2,1)} %get-tuple-element.4, bf16[8192,2048]{1,0:T(8,128)(2,1)} %all-gather.5.cloned.1.call-done), kind=kOutput, calls=%fused_computation.19 | convolution fusion | flops 11811160064 | bytes 42205184 | tf_op jit(solution)/shard_map/dot_general | solution.py:28
  480.7 24.8 %fusion.8 = f32[352,2048]{1,0:T(8,128)} fusion(bf16[8192,2048]{1,0:T(8,128)(2,1)} %all-gather.3.cloned.1.call-done, bf16[8192,352]{0,1:T(8,128)(2,1)} %convolution_convert_fusion.1, bf16[8192,352]{0,1:T(8,128)(2,1)} %convolution_convert_fusion), kind=kOutput, calls=%fused_computation.17 | convolution fusion | flops 11834228736 | bytes 47972352 | tf_op jit(solution)/shard_map/dot_general | solution.py:21
  505.5 0.0 copy-start.1
  505.5 23.6 %convolution_bitcast_fusion = f32[2048,352]{0,1:T(8,128)} fusion(bf16[8192,2048]{1,0:T(8,128)(2,1)} %all-gather.5.cloned.1.call-done, f32[8192,352]{0,1:T(8,128)} %get-tuple-element.5, bf16[8192,352]{0,1:T(8,128)(2,1)} %convolution_convert_fusion), kind=kOutput, calls=%fused_computation.18 | convolution fusion | flops 11831345152 | bytes 53739520 | tf_op jit(solution)/shard_map/dot_general | solution.py:29
  529.1 110.2 %reduce-scatter.2.cloned.1.call-done = bf16[512,2048]{1,0:T(8,128)(2,1)} async-done(((bf16[8192,2048]{1,0:T(8,128)(2,1)}), bf16[512,2048]{1,0:T(8,128)(2,1)}) %reduce-scatter.2.cloned.1.call-update) | async-done | bytes 2097168 | tf_op jit(solution)/shard_map/reduce_scatter | solution.py:27
  639.3 0.0 copy-done.1
Async XLA Ops:
  7.2 178.6 %copy-start = (bf16[2048,352]{0,1:T(8,128)(2,1)S(1)}, bf16[2048,352]{0,1:T(8,128)(2,1)}, u32[]{:S(2)}) copy-start(bf16[2048,352]{0,1:T(8,128)(2,1)} %param.7) | copy-start | bytes 4325380
  7.2 178.5 %all-gather.5.cloned.1.call-start = ((), (), s32[]{:S(2)}) async-start(), calls=%async_computation.2 | async-start | bytes 35651584 | tf_op jit(solution)/shard_map/all_gather | solution.py:12
  8.0 349.0 %all-gather.3.cloned.1.call-start = ((), (), s32[]{:S(2)}) async-start(), calls=%async_computation.1 | async-start | bytes 35651584 | tf_op jit(solution)/shard_map/all_gather | solution.py:15
  8.8 196.6 %copy-start.2 = (bf16[2048,352]{0,1:T(8,128)(2,1)S(1)}, bf16[2048,352]{0,1:T(8,128)(2,1)}, u32[]{:S(2)}) copy-start(bf16[2048,352]{0,1:T(8,128)(2,1)} %param.8) | copy-start | bytes 4325380
  8.8 630.4 %reduce-scatter.2.cloned.1.call-start = ((), (), s32[]{:S(2)}) async-start(), calls=%async_computation.3 | async-start | bytes 35651584 | tf_op jit(solution)/shard_map/reduce_scatter | solution.py:27
  505.5 133.7 %copy-start.1 = (bf16[2048,352]{0,1:T(8,128)(2,1)S(1)}, bf16[2048,352]{0,1:T(8,128)(2,1)}, u32[]{:S(2)}) copy-start(bf16[2048,352]{0,1:T(8,128)(2,1)} %param.7) | copy-start | bytes 4325380
Sparse Core Ops, SparseCore 0:
  9.7 176.0 all-gather.4
  187.4 169.5 all-gather.2
  460.1 179.0 reduce-scatter.1
where the time goes:
time: 654 us; the launch traced here: 646 us
  waiting for transfers between devices  420 us (64%)
  matrix products  211 us (32%)
  between operations  14.2 us (2%)
    all_gather x1, waiting for transfers between devices, device_step(): x_all = lax.all_gather(x_shard, 'tp', axis=0, tiled=True)  177 us
    all_gather x1, waiting for transfers between devices, device_step(): dy_all = lax.all_gather(dy_shard, 'tp', axis=0, tiled=True)  132 us
    reduce_scatter x1, waiting for transfers between devices, device_step(): lax.psum_scatter(partial_x.astype(jnp.bfloat16), 'tp', scatter_dimension=...  110 us
    dot_general x1, matrix products, device_step(): lax.dot_general(grad_up, w_up, contract_cols, preferred_element_type=jnp....  46.4 us
    dot_general x1, matrix products, device_step(): lax.dot_general(grad_gate, w_gate, contract_cols, preferred_element_type=...  28.3 us
    dot_general x1, matrix products, device_step(): lax.dot_general(dy_all, w_down, contract_cols, preferred_element_type=jnp...  28.3 us
    dot_general x1, matrix products, device_step(): lax.dot_general(mid_act, dy_all, contract_rows, preferred_element_type=jn...  24.8 us
    dot_general x1, matrix products, device_step(): lax.dot_general(x_all, grad_up, contract_rows, preferred_element_type=jnp...  23.6 us
  transfers between devices with their start and end apart: 3, of which 3 were waited for; matrix products, arithmetic and copies ran while one was open for 17% of the time, Pallas kernels for 0%

commit v1 on v0

v1 whole, which is shorter than its diff:
```python
import jax
import jax.numpy as jnp
from jax import lax
from jax.experimental import pallas as pl
from jax.experimental.pallas import tpu as pltpu
from jax.sharding import PartitionSpec as P


F32, BF16 = jnp.float32, jnp.bfloat16
BLOCK = 512
LANES = 128


def token_kernel(has_received, x_ref, dy_ref, w_in_ref, w_down_ref, w_back_ref, *refs):
    received_ref, (mid_ref, grad_ref, part_ref) = (refs[0], refs[1:]) if has_received else (None, refs)
    width = mid_ref.shape[1]
    pre = jnp.dot(x_ref[...], w_in_ref[...], preferred_element_type=F32).astype(BF16).astype(F32)
    gate, up = pre[:, :width], pre[:, width:]
    grad_mid = jnp.dot(dy_ref[...], w_down_ref[...], preferred_element_type=F32)
    sig = jax.nn.sigmoid(gate)
    act = gate * sig
    mid_ref[...] = (act * up).astype(BF16)
    grad_ref[:, :width] = (grad_mid * up * sig * (1.0 + gate * (1.0 - sig))).astype(BF16)
    grad_ref[:, width:] = (grad_mid * act).astype(BF16)
    part = jnp.dot(grad_ref[...], w_back_ref[...], preferred_element_type=F32)
    if has_received:
        part = part + received_ref[...].astype(F32)
    part_ref[...] = part.astype(BF16)


def token_call(x, dy, w_in, w_down, w_back, received=None):
    rows, hidden = x.shape
    width = w_down.shape[1]
    block = min(BLOCK, rows)
    tokens = lambda n: pl.BlockSpec((block, n), lambda i: (i, 0))
    whole = lambda a: pl.BlockSpec(a.shape, lambda i: (0, 0))
    args = [x, dy, w_in, w_down, w_back] + ([] if received is None else [received])
    specs = [tokens(hidden), tokens(hidden), whole(w_in), whole(w_down), whole(w_back)]
    specs += [] if received is None else [tokens(hidden)]
    return pl.pallas_call(
        lambda *refs: token_kernel(received is not None, *refs),
        grid=(rows // block,),
        in_specs=specs,
        out_specs=[tokens(width), tokens(2 * width), tokens(hidden)],
        out_shape=[jax.ShapeDtypeStruct((rows, n), BF16) for n in (width, 2 * width, hidden)],
        compiler_params=pltpu.CompilerParams(dimension_semantics=("arbitrary",), vmem_limit_bytes=60 * 2**20),
        cost_estimate=pl.CostEstimate(flops=10 * rows * hidden * width, bytes_accessed=8 * rows * hidden,
                                      transcendentals=rows * width),
        name="token_part",
    )(*args)


def weight_kernel(has_acc, x_ref, dy_ref, mid_ref, grad_ref, *refs):
    acc_refs, outs = (refs[:3], refs[3:]) if has_acc else ((), refs)
    inner, width = outs[0].shape[0], mid_ref.shape[1]

    @pl.when(pl.program_id(0) == 0)
    def _():
        if has_acc:
            for acc, out in zip(acc_refs, outs):
                pltpu.sync_copy(acc, out)
        else:
            for out in outs:
                out[...] = jnp.zeros_like(out)

    rows_by_rows = (((0,), (0,)), ((), ()))
    for out, left, right in ((outs[0], grad_ref[:, :width], x_ref), (outs[1], grad_ref[:, width:], x_ref),
                             (outs[2], mid_ref[...], dy_ref)):
        term = lax.dot_general(left, right[...], rows_by_rows, preferred_element_type=F32)
        out[...] += term[:inner]


def weight_call(x, dy, mid, grad, inner, acc):
    rows, hidden = x.shape
    width = mid.shape[1]
    block = min(BLOCK, rows)
    tokens = lambda n: pl.BlockSpec((block, n), lambda i: (i, 0))
    return pl.pallas_call(
        lambda *refs: weight_kernel(acc is not None, *refs),
        grid=(rows // block,),
        in_specs=[tokens(hidden), tokens(hidden), tokens(width), tokens(2 * width)]
        + ([] if acc is None else [pl.BlockSpec(memory_space=pl.ANY)] * 3),
        out_specs=[pl.BlockSpec((inner, hidden), lambda i: (0, 0))] * 3,
        out_shape=[jax.ShapeDtypeStruct((inner, hidden), F32)] * 3,
        compiler_params=pltpu.CompilerParams(dimension_semantics=("arbitrary",), vmem_limit_bytes=60 * 2**20),
        cost_estimate=pl.CostEstimate(flops=6 * rows * hidden * width,
                                      bytes_accessed=4 * rows * hidden + 24 * inner * hidden, transcendentals=0),
        name="weight_part",
    )(x, dy, mid, grad, *(() if acc is None else acc))


def after(value, *earlier):
    return lax.optimization_barrier((value, *earlier))[0]


def solution(mesh):
    tp = mesh.shape["tp"]
    rings = [list(range(core, tp, 2)) for core in range(2)]
    swap = [(i, i ^ 1) for i in range(tp)]

    def gather(shard):
        return lax.all_gather(shard, "tp", axis=0, tiled=True, axis_index_groups=rings)

    def scatter(part):
        return lax.psum_scatter(part, "tp", scatter_dimension=0, tiled=True, axis_index_groups=rings)

    def swapped(value):
        return lax.ppermute(value, "tp", swap)

    def device_step(x_shard, dy_shard, w_gate, w_up, w_down):
        rows, inner = x_shard.shape[0], w_down.shape[0]
        cut = rows * 5 // 8
        pad = -inner % LANES
        w_in = jnp.concatenate([jnp.pad(w, ((0, 0), (0, pad))) for w in (w_gate, w_up)], axis=1)
        w_back = jnp.concatenate([jnp.pad(w.T, ((0, pad), (0, 0))) for w in (w_gate, w_up)], axis=0)
        w_mid = jnp.pad(w_down.T, ((0, 0), (0, pad)))
        weights = (w_in, w_mid, w_back)

        x0 = gather(x_shard[:cut])
        dy0 = gather(dy_shard[:cut])
        x1 = gather(x_shard[cut:])
        dy1 = gather(dy_shard[cut:])
        x0_other, dy0_other, x1_other, dy1_other = (swapped(a) for a in (x0, dy0, x1, dy1))

        *rest0_other, part0_other = token_call(x0_other, dy0_other, *weights)
        *rest0, part0 = token_call(x0, dy0, *weights, swapped(part0_other))
        sum0 = scatter(part0)
        acc = weight_call(x0_other, after(dy0_other, part0), *rest0_other, inner, None)

        *rest1_other, part1_other = token_call(x1_other, dy1_other, after(w_in, acc[0]), w_mid, w_back)
        *rest1, part1 = token_call(x1, dy1, *weights, swapped(part1_other))
        sum1 = scatter(part1)
        acc = weight_call(x0, after(dy0, part1), *rest0, inner, acc)
        acc = weight_call(x1_other, dy1_other, *rest1_other, inner, acc)
        acc = weight_call(x1, dy1, *rest1, inner, acc)
        return jnp.concatenate([sum0, sum1], axis=0), acc[0].T, acc[1].T, acc[2]

    tok_spec = P(("dp", "tp"), None)
    col_spec = P(None, "tp")
    grad_col_spec = P("dp", "tp")
    return jax.shard_map(device_step, mesh=mesh,
                         in_specs=(tok_spec, tok_spec, col_spec, col_spec, P("tp", None)),
                         out_specs=(tok_spec, grad_col_spec, grad_col_spec, tok_spec),
                         check_vma=False)
```

time: 654 us -> 681 us (1.041); the launches traced: 646 us -> 681 us
  matrix products: 211 us -> 0 us
  Pallas kernels: 0 us -> 193 us
  waiting for transfers between devices: 420 us -> 445 us
  local copies, waits for them, and re-layouts: 0.02 us -> 17.1 us
  other arithmetic: 0 us -> 6.88 us
    dot_general x8 -> x0, matrix products: 211 us -> none  [the longest x1 46.4 us: device_step(): lax.dot_general(grad_up, w_up, contract_cols, preferred_element_type=jnp....]
    pallas_call x0 -> x8, Pallas kernels: none -> 193 us  [the longest x4 111 us: token_call(): pl.pallas_call(lambda *refs: token_kernel(received is not None, *refs), g...]
    ppermute x0 -> x6, waiting for transfers between devices: none -> 11.6 us  [swapped(): return lax.ppermute(value, 'tp', swap)]
    slice x0 -> x4, local copies, waits for them, and re-layouts: none -> 8.06 us  [the longest x1 2.66 us: device_step(): x0 = gather(x_shard[:cut])]
    reduce_scatter x1 -> x2, waiting for transfers between devices: 110 us -> 118 us  [scatter(): lax.psum_scatter(part, 'tp', scatter_dimension=0, tiled=True, axis_index_...]
    concatenate x0 -> x3, other arithmetic: none -> 6.88 us  [the longest x1 3.13 us: device_step(): return (jnp.concatenate([sum0, sum1], axis=0), acc[0].T, acc[1].T, acc[2])]
    all_gather x2 -> x4, waiting for transfers between devices: 309 us -> 315 us  [gather(): lax.all_gather(shard, 'tp', axis=0, tiled=True, axis_index_groups=rings)]
  transfers between devices with their start and end apart: 3 -> 12, of which waited for: 3 -> 8; matrix products, arithmetic and copies ran while one was open for 17% -> 3% of each run, Pallas kernels for 0% -> 22%
where the time goes in v1:
time: 681 us
  waiting for transfers between devices  445 us (65%)
  Pallas kernels  193 us (28%)
  local copies, waits for them, and re-layouts  17.1 us (3%)
  between operations  14.2 us (2%)
  other arithmetic  6.88 us (1%)
    all_gather x4, waiting for transfers between devices, gather(): lax.all_gather(shard, 'tp', axis=0, tiled=True, axis_index_groups=rings)  315 us
    reduce_scatter x2, waiting for transfers between devices, scatter(): lax.psum_scatter(part, 'tp', scatter_dimension=0, tiled=True, axis_index_...  118 us
    pallas_call x4, Pallas kernels, token_call(): pl.pallas_call(lambda *refs: token_kernel(received is not None, *refs), g...  111 us
    pallas_call x4, Pallas kernels, weight_call(): pl.pallas_call(lambda *refs: weight_kernel(acc is not None, *refs), grid=...  81.9 us
  transfers between devices with their start and end apart: 12, of which 8 were waited for; matrix products, arithmetic and copies ran while one was open for 3% of the time, Pallas kernels for 22%

profile of v1, /device:TPU:21, one launch (start us, length us, event | category | flops | bytes accessed | tf_op | source)
XLA Modules:
  0.0 680.7 jit_solution(18018798817150509508)
XLA Ops:
  7.2 0.0 copy-start.3
  7.2 0.1 all-gather.5.cloned.1.call-start
  7.3 2.7 slice.12
  9.9 0.1 all-gather.5.cloned.1.call-update
  10.0 0.1 all-gather.7.cloned.1.call-start
  10.1 1.1 slice.13
  11.2 0.1 all-gather.7.cloned.1.call-update
  11.3 0.1 all-gather.9.cloned.1.call-start
  11.3 2.2 slice.14
  13.5 0.1 all-gather.9.cloned.1.call-update
  13.6 0.1 all-gather.11.cloned.1.call-start
  13.6 111.5 %all-gather.5.cloned.1.call-done.refs_0_ = bf16[2560,2048]{1,0:T(8,128)(2,1)} async-done(((bf16[320,2048]{1,0:T(8,128)(2,1)}), bf16[2560,2048]{1,0:T(8,128)(2,1)}) %all-gather.5.cloned.1.call-update) | async-done | bytes 10485776 | tf_op jit(solution)/shard_map/all_gather | solution.py:102
  125.1 0.8 collective-permute-start
  126.0 110.4 %all-gather.7.cloned.1.call-done.refs_1_ = bf16[2560,2048]{1,0:T(8,128)(2,1)} async-done(((bf16[320,2048]{1,0:T(8,128)(2,1)}), bf16[2560,2048]{1,0:T(8,128)(2,1)}) %all-gather.7.cloned.1.call-update) | async-done | bytes 10485776 | tf_op jit(solution)/shard_map/all_gather | solution.py:102
  236.4 0.8 collective-permute-start.1
  237.2 2.1 slice.15
  239.3 0.1 all-gather.11.cloned.1.call-update
  239.4 0.1 reduce-scatter.5.cloned.1.call-start
  239.4 0.9 copy.10
  240.3 1.9 copy.9
  242.2 2.6 copy.11
  244.7 2.8 pad.19.refs_3_
  247.5 2.0 fusion.5.refs_2_
  249.5 1.0 copy-done.2
  250.4 1.8 fusion.4.refs_4_
  252.2 0.0 collective-permute-done.refs_0_
  252.2 1.1 collective-permute-done.1.refs_1_
  253.3 32.7 %token_part.4 = (bf16[2560,384]{1,0:T(8,128)(2,1)}, bf16[2560,768]{1,0:T(8,128)(2,1)}, bf16[2560,2048]{1,0:T(8,128)(2,1)}) custom-call(bf16[2560,2048]{1,0:T(8,128)(2,1)} %collective-permute-done.refs_0_, bf16[2560,2048]{1,0:T(8,128)(2,1)} %collective-permute-done.1.refs_1_, bf16[2048,768]{1,0:T(8,128)(2,1)} %fusion.5.refs_2_, ...), custom_call_target="tpu_custom_call" | custom-call | flops 20132659200 | bytes 41943040 | tf_op jit(solution)/shard_map/token_part/pallas_call | solution.py:40
  286.0 0.4 collective-permute-start.2
  286.4 21.9 %all-gather.9.cloned.1.call-done.refs_0_ = bf16[1536,2048]{1,0:T(8,128)(2,1)} async-done(((bf16[192,2048]{1,0:T(8,128)(2,1)}), bf16[1536,2048]{1,0:T(8,128)(2,1)}) %all-gather.9.cloned.1.call-update) | async-done | bytes 6291472 | tf_op jit(solution)/shard_map/all_gather | solution.py:102
  308.3 0.8 collective-permute-start.3
  309.1 70.9 %all-gather.11.cloned.1.call-done.refs_1_ = bf16[1536,2048]{1,0:T(8,128)(2,1)} async-done(((bf16[192,2048]{1,0:T(8,128)(2,1)}), bf16[1536,2048]{1,0:T(8,128)(2,1)}) %all-gather.11.cloned.1.call-update) | async-done | bytes 6291472 | tf_op jit(solution)/shard_map/all_gather | solution.py:102
  380.0 0.8 collective-permute-start.4
  380.9 33.8 %token_part.5 = (bf16[2560,384]{1,0:T(8,128)(2,1)}, bf16[2560,768]{1,0:T(8,128)(2,1)}, bf16[2560,2048]{1,0:T(8,128)(2,1)}) custom-call(bf16[2560,2048]{1,0:T(8,128)(2,1)} %all-gather.5.cloned.1.call-done.refs_0_, bf16[2560,2048]{1,0:T(8,128)(2,1)} %all-gather.7.cloned.1.call-done.refs_1_, bf16[2048,768]{1,0:T(8,128)(2,1)} %fusion.5.refs_2_, ...), custom_call_target="tpu_custom_call" | custom-call | flops 20132659200 | bytes 41943040 | tf_op jit(solution)/shard_map/token_part/pallas_call | solution.py:40
  414.7 18.2 %weight_part.4 = (f32[352,2048]{1,0:T(8,128)}, f32[352,2048]{1,0:T(8,128)}, f32[352,2048]{1,0:T(8,128)}) custom-call(bf16[2560,2048]{1,0:T(8,128)(2,1)} %collective-permute-done.refs_0_, bf16[2560,2048]{1,0:T(8,128)(2,1)} %collective-permute-done.1.refs_1_, bf16[2560,384]{1,0:T(8,128)(2,1)} %get-tuple-element.34.refs_2_, ...), custom_call_target="tpu_custom_call" | custom-call | flops 12079595520 | bytes 38273024 | tf_op jit(solution)/shard_map/weight_part/pallas_call | solution.py:78
  432.9 21.9 %token_part.6 = (bf16[1536,384]{1,0:T(8,128)(2,1)}, bf16[1536,768]{1,0:T(8,128)(2,1)}, bf16[1536,2048]{1,0:T(8,128)(2,1)}) custom-call(bf16[1536,2048]{1,0:T(8,128)(2,1)} %collective-permute-done.3.refs_0_, bf16[1536,2048]{1,0:T(8,128)(2,1)} %collective-permute-done.4.refs_1_, bf16[2048,768]{1,0:T(8,128)(2,1)} %fusion.5.refs_2_, ...), custom_call_target="tpu_custom_call" | custom-call | flops 12079595520 | bytes 25165824 | tf_op jit(solution)/shard_map/token_part/pallas_call | solution.py:40
  454.8 0.0 collective-permute-start.5
  454.8 10.5 %collective-permute-done.5.refs_5_ = bf16[1536,2048]{1,0:T(8,128)(2,1)} collective-permute-done((bf16[1536,2048]{1,0:T(8,128)(2,1)}, bf16[1536,2048]{1,0:T(8,128)(2,1)}, u32[]{:S(2)}, u32[]{:S(2)}) %collective-permute-start.5) | collective-permute-done | bytes 6291488 | tf_op jit(solution)/shard_map/ppermute | solution.py:108
  465.3 23.1 %token_part.7 = (bf16[1536,384]{1,0:T(8,128)(2,1)}, bf16[1536,768]{1,0:T(8,128)(2,1)}, bf16[1536,2048]{1,0:T(8,128)(2,1)}) custom-call(bf16[1536,2048]{1,0:T(8,128)(2,1)} %all-gather.9.cloned.1.call-done.refs_0_, bf16[1536,2048]{1,0:T(8,128)(2,1)} %all-gather.11.cloned.1.call-done.refs_1_, bf16[2048,768]{1,0:T(8,128)(2,1)} %fusion.5.refs_2_, ...), custom_call_target="tpu_custom_call" | custom-call | flops 12079595520 | bytes 25165824 | tf_op jit(solution)/shard_map/token_part/pallas_call | solution.py:40
  488.4 0.1 reduce-scatter.5.cloned.1.call-update
  488.4 0.1 reduce-scatter.3.cloned.1.call-start
  488.5 0.6 reduce-scatter.3.cloned.1.call-update
  489.1 25.0 %weight_part.5 = (f32[352,2048]{1,0:T(8,128)}, f32[352,2048]{1,0:T(8,128)}, f32[352,2048]{1,0:T(8,128)}) custom-call(bf16[2560,2048]{1,0:T(8,128)(2,1)} %all-gather.5.cloned.1.call-done.refs_0_, bf16[2560,2048]{1,0:T(8,128)(2,1)} %all-gather.7.cloned.1.call-done.refs_1_, bf16[2560,384]{1,0:T(8,128)(2,1)} %get-tuple-element.45.refs_2_, ...), custom_call_target="tpu_custom_call" | custom-call | flops 12079595520 | bytes 38273024 | tf_op jit(solution)/shard_map/weight_part/pallas_call | solution.py:78
  514.0 19.3 %weight_part.6 = (f32[352,2048]{1,0:T(8,128)}, f32[352,2048]{1,0:T(8,128)}, f32[352,2048]{1,0:T(8,128)}) custom-call(bf16[1536,2048]{1,0:T(8,128)(2,1)} %collective-permute-done.3.refs_0_, bf16[1536,2048]{1,0:T(8,128)(2,1)} %collective-permute-done.4.refs_1_, bf16[1536,384]{1,0:T(8,128)(2,1)} %get-tuple-element.42.refs_2_, ...), custom_call_target="tpu_custom_call" | custom-call | flops 7247757312 | bytes 29884416 | tf_op jit(solution)/shard_map/weight_part/pallas_call | solution.py:78
  533.4 19.4 %weight_part.7 = (f32[352,2048]{1,0:T(8,128)}, f32[352,2048]{1,0:T(8,128)}, f32[352,2048]{1,0:T(8,128)}) custom-call(bf16[1536,2048]{1,0:T(8,128)(2,1)} %all-gather.9.cloned.1.call-done.refs_0_, bf16[1536,2048]{1,0:T(8,128)(2,1)} %all-gather.11.cloned.1.call-done.refs_1_, bf16[1536,384]{1,0:T(8,128)(2,1)} %get-tuple-element.40.refs_2_, ...), custom_call_target="tpu_custom_call" | custom-call | flops 7247757312 | bytes 29884416 | tf_op jit(solution)/shard_map/weight_part/pallas_call | solution.py:78
  552.8 5.7 reduce-scatter.5.cloned.1.call-done
  558.5 112.3 %reduce-scatter.3.cloned.1.call-done = bf16[320,2048]{1,0:T(8,128)(2,1)} async-done(((bf16[2560,2048]{1,0:T(8,128)(2,1)}), bf16[320,2048]{1,0:T(8,128)(2,1)}) %reduce-scatter.3.cloned.1.call-update) | async-done | bytes 1310736 | tf_op jit(solution)/shard_map/reduce_scatter | solution.py:105
  670.8 3.1 pad_maximum_fusion
  (9 shorter events, 0.0 us)
Async XLA Ops:
  7.2 2.9 copy-start.3
  7.2 118.0 %all-gather.5.cloned.1.call-start = ((), (), s32[]{:S(2)}) async-start(), calls=%async_computation.2 | async-start | bytes 11796480 | tf_op jit(solution)/shard_map/all_gather | solution.py:102
  10.0 226.4 %all-gather.7.cloned.1.call-start = ((), (), s32[]{:S(2)}) async-start(), calls=%async_computation.3 | async-start | bytes 11796480 | tf_op jit(solution)/shard_map/all_gather | solution.py:102
  11.2 228.2 %copy-start = (bf16[2048,352]{0,1:T(8,128)(2,1)S(1)}, bf16[2048,352]{0,1:T(8,128)(2,1)}, u32[]{:S(2)}) copy-start(bf16[2048,352]{0,1:T(8,128)(2,1)} %param.8) | copy-start | bytes 4325380
  11.3 297.0 %all-gather.9.cloned.1.call-start = ((), (), s32[]{:S(2)}) async-start(), calls=%async_computation.5 | async-start | bytes 7077888 | tf_op jit(solution)/shard_map/all_gather | solution.py:102
  13.6 366.5 %all-gather.11.cloned.1.call-start = ((), (), s32[]{:S(2)}) async-start(), calls=%async_computation.6 | async-start | bytes 7077888 | tf_op jit(solution)/shard_map/all_gather | solution.py:102
  125.1 127.1 %collective-permute-start = (bf16[2560,2048]{1,0:T(8,128)(2,1)}, bf16[2560,2048]{1,0:T(8,128)(2,1)}, u32[]{:S(2)}, u32[]{:S(2)}) collective-permute-start(bf16[2560,2048]{1,0:T(8,128)(2,1)} %all-gather.5.cloned.1.call-done.refs_0_), channel_id=1, source_target_pairs={{0,1},{1,0},{2,3},{3,2},{4,5},{5,4},{6,7},{7,6},{8,9},{9,8},{10,11... | collective-permute-start | bytes 31457288 | tf_op jit(solution)/shard_map/ppermute | solution.py:108
  236.4 17.0 %collective-permute-start.1 = (bf16[2560,2048]{1,0:T(8,128)(2,1)}, bf16[2560,2048]{1,0:T(8,128)(2,1)}, u32[]{:S(2)}, u32[]{:S(2)}) collective-permute-start(bf16[2560,2048]{1,0:T(8,128)(2,1)} %all-gather.7.cloned.1.call-done.refs_1_), channel_id=1, source_target_pairs={{0,1},{1,0},{2,3},{3,2},{4,5},{5,4},{6,7},{7,6},{8,9},{9,8},{10,11... | collective-permute-start | bytes 31457288 | tf_op jit(solution)/shard_map/ppermute | solution.py:108
  239.4 319.1 %reduce-scatter.5.cloned.1.call-start = ((), (), s32[]{:S(2)}) async-start(), calls=%async_computation.7 | async-start | bytes 7077888 | tf_op jit(solution)/shard_map/reduce_scatter | solution.py:105
  247.5 2.0 copy-start.1
  247.5 2.9 copy-start.2
  286.0 94.9 %collective-permute-start.2 = (bf16[2560,2048]{1,0:T(8,128)(2,1)}, bf16[2560,2048]{1,0:T(8,128)(2,1)}, u32[]{:S(2)}, u32[]{:S(2)}) collective-permute-start(bf16[2560,2048]{1,0:T(8,128)(2,1)} %get-tuple-element.31), channel_id=1, source_target_pairs={{0,1},{1,0},{2,3},{3,2},{4,5},{5,4},{6,7},{7,6},{8,9},{9,8},{10,11... | collective-permute-start | bytes 31457288 | tf_op jit(solution)/shard_map/ppermute | solution.py:108
  308.3 124.6 %collective-permute-start.3 = (bf16[1536,2048]{1,0:T(8,128)(2,1)}, bf16[1536,2048]{1,0:T(8,128)(2,1)}, u32[]{:S(2)}, u32[]{:S(2)}) collective-permute-start(bf16[1536,2048]{1,0:T(8,128)(2,1)} %all-gather.9.cloned.1.call-done.refs_0_), channel_id=1, source_target_pairs={{0,1},{1,0},{2,3},{3,2},{4,5},{5,4},{6,7},{7,6},{8,9},{9,8},{10,11... | collective-permute-start | bytes 18874376 | tf_op jit(solution)/shard_map/ppermute | solution.py:108
  380.0 52.9 %collective-permute-start.4 = (bf16[1536,2048]{1,0:T(8,128)(2,1)}, bf16[1536,2048]{1,0:T(8,128)(2,1)}, u32[]{:S(2)}, u32[]{:S(2)}) collective-permute-start(bf16[1536,2048]{1,0:T(8,128)(2,1)} %all-gather.11.cloned.1.call-done.refs_1_), channel_id=1, source_target_pairs={{0,1},{1,0},{2,3},{3,2},{4,5},{5,4},{6,7},{7,6},{8,9},{9,8},{10,11... | collective-permute-start | bytes 18874376 | tf_op jit(solution)/shard_map/ppermute | solution.py:108
  454.8 10.5 %collective-permute-start.5 = (bf16[1536,2048]{1,0:T(8,128)(2,1)}, bf16[1536,2048]{1,0:T(8,128)(2,1)}, u32[]{:S(2)}, u32[]{:S(2)}) collective-permute-start(bf16[1536,2048]{1,0:T(8,128)(2,1)} %get-tuple-element.38), channel_id=1, source_target_pairs={{0,1},{1,0},{2,3},{3,2},{4,5},{5,4},{6,7},{7,6},{8,9},{9,8},{10,11... | collective-permute-start | bytes 18874376 | tf_op jit(solution)/shard_map/ppermute | solution.py:108
  488.4 182.3 %reduce-scatter.3.cloned.1.call-start = ((), (), s32[]{:S(2)}) async-start(), calls=%async_computation.4 | async-start | bytes 11796480 | tf_op jit(solution)/shard_map/reduce_scatter | solution.py:105
Sparse Core Ops, SparseCore 0:
  10.2 114.9 all-gather.4
  127.3 109.0 all-gather.6
  238.5 69.7 all-gather.8
  310.3 69.7 all-gather.10
  488.6 69.8 reduce-scatter.4
  560.7 110.0 reduce-scatter.2

commit v2 on v1

--- a/solution.py
+++ b/solution.py
@@ -7,16 +7,20 @@
 
 
 F32, BF16 = jnp.float32, jnp.bfloat16
-BLOCK = 512
+SHARDS = 2
 LANES = 128
+
+
+def flat(ref):
+    return ref[...].reshape(-1, ref.shape[-1])
 
 
 def token_kernel(has_received, x_ref, dy_ref, w_in_ref, w_down_ref, w_back_ref, *refs):
     received_ref, (mid_ref, grad_ref, part_ref) = (refs[0], refs[1:]) if has_received else (None, refs)
     width = mid_ref.shape[1]
-    pre = jnp.dot(x_ref[...], w_in_ref[...], preferred_element_type=F32).astype(BF16).astype(F32)
+    pre = jnp.dot(flat(x_ref), w_in_ref[...], preferred_element_type=F32).astype(BF16).astype(F32)
     gate, up = pre[:, :width], pre[:, width:]
-    grad_mid = jnp.dot(dy_ref[...], w_down_ref[...], preferred_element_type=F32)
+    grad_mid = jnp.dot(flat(dy_ref), w_down_ref[...], preferred_element_type=F32)
     sig = jax.nn.sigmoid(gate)
     act = gate * sig
     mid_ref[...] = (act * up).astype(BF16)
@@ -28,18 +32,23 @@
     part_ref[...] = part.astype(BF16)
 
 
-def token_call(x, dy, w_in, w_down, w_back, received=None):
-    rows, hidden = x.shape
+def halves(both):
+    _, _, rows, hidden = both.shape
+    return [pl.BlockSpec((SHARDS, None, rows, hidden), lambda i, part=part: (i, part, 0, 0)) for part in range(2)]
+
+
+def token_call(both, w_in, w_down, w_back, received=None):
+    shards, _, shard_rows, hidden = both.shape
+    rows, block = shards * shard_rows, SHARDS * shard_rows
     width = w_down.shape[1]
-    block = min(BLOCK, rows)
     tokens = lambda n: pl.BlockSpec((block, n), lambda i: (i, 0))
     whole = lambda a: pl.BlockSpec(a.shape, lambda i: (0, 0))
-    args = [x, dy, w_in, w_down, w_back] + ([] if received is None else [received])
-    specs = [tokens(hidden), tokens(hidden), whole(w_in), whole(w_down), whole(w_back)]
+    args = [both, both, w_in, w_down, w_back] + ([] if received is None else [received])
+    specs = halves(both) + [whole(w_in), whole(w_down), whole(w_back)]
     specs += [] if received is None else [tokens(hidden)]
     return pl.pallas_call(
         lambda *refs: token_kernel(received is not None, *refs),
-        grid=(rows // block,),
+        grid=(shards // SHARDS,),
         in_specs=specs,
         out_specs=[tokens(width), tokens(2 * width), tokens(hidden)],
         out_shape=[jax.ShapeDtypeStruct((rows, n), BF16) for n in (width, 2 * width, hidden)],
@@ -66,19 +75,19 @@
     rows_by_rows = (((0,), (0,)), ((), ()))
     for out, left, right in ((outs[0], grad_ref[:, :width], x_ref), (outs[1], grad_ref[:, width:], x_ref),
                              (outs[2], mid_ref[...], dy_ref)):
-        term = lax.dot_general(left, right[...], rows_by_rows, preferred_element_type=F32)
+        term = lax.dot_general(left, flat(right), rows_by_rows, preferred_element_type=F32)
         out[...] += term[:inner]
 
 
-def weight_call(x, dy, mid, grad, inner, acc):
-    rows, hidden = x.shape
+def weight_call(both, mid, grad, inner, acc):
+    shards, _, shard_rows, hidden = both.shape
+    rows, block = shards * shard_rows, SHARDS * shard_rows
     width = mid.shape[1]
-    block = min(BLOCK, rows)
     tokens = lambda n: pl.BlockSpec((block, n), lambda i: (i, 0))
     return pl.pallas_call(
         lambda *refs: weight_kernel(acc is not None, *refs),
-        grid=(rows // block,),
-        in_specs=[tokens(hidden), tokens(hidden), tokens(width), tokens(2 * width)]
+        grid=(shards // SHARDS,),
+        in_specs=halves(both) + [tokens(width), tokens(2 * width)]
         + ([] if acc is None else [pl.BlockSpec(memory_space=pl.ANY)] * 3),
         out_specs=[pl.BlockSpec((inner, hidden), lambda i: (0, 0))] * 3,
         out_shape=[jax.ShapeDtypeStruct((inner, hidden), F32)] * 3,
@@ -86,7 +95,7 @@
         cost_estimate=pl.CostEstimate(flops=6 * rows * hidden * width,
                                       bytes_accessed=4 * rows * hidden + 24 * inner * hidden, transcendentals=0),
         name="weight_part",
-    )(x, dy, mid, grad, *(() if acc is None else acc))
+    )(both, both, mid, grad, *(() if acc is None else acc))
 
 
 def after(value, *earlier):
@@ -98,8 +107,9 @@
     rings = [list(range(core, tp, 2)) for core in range(2)]
     swap = [(i, i ^ 1) for i in range(tp)]
 
-    def gather(shard):
-        return lax.all_gather(shard, "tp", axis=0, tiled=True, axis_index_groups=rings)
+    def gather(x, dy):
+        both = lax.all_gather(jnp.concatenate([x, dy], axis=0), "tp", axis=0, tiled=True, axis_index_groups=rings)
+        return both.reshape(-1, 2, *x.shape)
 
     def scatter(part):
         return lax.psum_scatter(part, "tp", scatter_dimension=0, tiled=True, axis_index_groups=rings)
@@ -116,24 +126,23 @@
         w_mid = jnp.pad(w_down.T, ((0, 0), (0, pad)))
         weights = (w_in, w_mid, w_back)
 
-        x0 = gather(x_shard[:cut])
-        dy0 = gather(dy_shard[:cut])
-        x1 = gather(x_shard[cut:])
-        dy1 = gather(dy_shard[cut:])
-        x0_other, dy0_other, x1_other, dy1_other = (swapped(a) for a in (x0, dy0, x1, dy1))
+        both0 = gather(x_shard[:cut], dy_shard[:cut])
+        both1 = gather(x_shard[cut:], dy_shard[cut:])
+        both0_other, both1_other = swapped(both0), swapped(both1)
 
-        *rest0_other, part0_other = token_call(x0_other, dy0_other, *weights)
-        *rest0, part0 = token_call(x0, dy0, *weights, swapped(part0_other))
+        *rest0_other, part0_other = token_call(both0_other, *weights)
+        *rest0, part0 = token_call(both0, *weights, swapped(part0_other))
         sum0 = scatter(part0)
-        acc = weight_call(x0_other, after(dy0_other, part0), *rest0_other, inner, None)
+        acc = weight_call(both0_other, *after(rest0_other, part0), inner, None)
 
-        *rest1_other, part1_other = token_call(x1_other, dy1_other, after(w_in, acc[0]), w_mid, w_back)
-        *rest1, part1 = token_call(x1, dy1, *weights, swapped(part1_other))
+        *rest1_other, part1_other = token_call(both1_other, after(w_in, acc[0]), w_mid, w_back)
+        *rest1, part1 = token_call(both1, *weights, swapped(part1_other))
         sum1 = scatter(part1)
-        acc = weight_call(x0, after(dy0, part1), *rest0, inner, acc)
-        acc = weight_call(x1_other, dy1_other, *rest1_other, inner, acc)
-        acc = weight_call(x1, dy1, *rest1, inner, acc)
-        return jnp.concatenate([sum0, sum1], axis=0), acc[0].T, acc[1].T, acc[2]
+        acc = weight_call(both0, *after(rest0, part1), inner, acc)
+        acc = weight_call(both1_other, *rest1_other, inner, acc)
+        acc = weight_call(both1, *rest1, inner, acc)
+        grad_x = lax.dynamic_update_slice(after(jnp.pad(sum0, ((0, rows - cut), (0, 0)))), sum1, (cut, 0))
+        return grad_x, acc[0].T, acc[1].T, acc[2]
 
     tok_spec = P(("dp", "tp"), None)
     col_spec = P(None, "tp")

time: 681 us -> 581 us (0.85)
  waiting for transfers between devices: 445 us -> 341 us
  Pallas kernels: 193 us -> 202 us
    reduce_scatter x2, waiting for transfers between devices: 118 us -> 34.8 us  [scatter(): lax.psum_scatter(part, 'tp', scatter_dimension=0, tiled=True, axis_index_...]
    all_gather x4 -> x2, waiting for transfers between devices: 315 us -> 279 us  [gather(): lax.all_gather(jnp.concatenate([x, dy], axis=0), 'tp', axis=0, tiled=True...]
    ppermute x6 -> x4, waiting for transfers between devices: 11.6 us -> 27 us  [swapped(): return lax.ppermute(value, 'tp', swap)]
    pallas_call x4, Pallas kernels: 81.9 us -> 91.2 us  [weight_call(): pl.pallas_call(lambda *refs: weight_kernel(acc is not None, *refs), grid=...]
  transfers between devices with their start and end apart: 12 -> 8, of which waited for: 8 -> 5; matrix products, arithmetic and copies ran while one was open for 3% -> 3% of each run, Pallas kernels for 22% -> 35%
where the time goes in v2:
time: 581 us
  waiting for transfers between devices  341 us (59%)
  Pallas kernels  202 us (35%)
  local copies, waits for them, and re-layouts  15.2 us (3%)
  between operations  13.9 us (2%)
  other arithmetic  6.64 us (1%)
    all_gather x2, waiting for transfers between devices, gather(): lax.all_gather(jnp.concatenate([x, dy], axis=0), 'tp', axis=0, tiled=True...  279 us
    pallas_call x4, Pallas kernels, token_call(): pl.pallas_call(lambda *refs: token_kernel(received is not None, *refs), g...  110 us
    pallas_call x4, Pallas kernels, weight_call(): pl.pallas_call(lambda *refs: weight_kernel(acc is not None, *refs), grid=...  91.2 us
    reduce_scatter x2, waiting for transfers between devices, scatter(): lax.psum_scatter(part, 'tp', scatter_dimension=0, tiled=True, axis_index_...  34.8 us
    ppermute x4, waiting for transfers between devices, swapped(): return lax.ppermute(value, 'tp', swap)  27 us
  transfers between devices with their start and end apart: 8, of which 5 were waited for; matrix products, arithmetic and copies ran while one was open for 3% of the time, Pallas kernels for 35%

profile of v2, /device:TPU:21, one launch (start us, length us, event | category | flops | bytes accessed | tf_op | source)
XLA Modules:
  0.0 580.7 jit_solution(15444901537665353572)
XLA Ops:
  7.2 0.0 slice-start
  7.2 0.0 slice-start.2
  7.2 0.1 all-gather.3.cloned.1.call-start
  7.3 1.2 slice-done
  8.5 0.4 slice-done.2
  8.9 1.7 pad_maximum_fusion
  10.6 0.1 all-gather.3.cloned.1.call-update
  10.6 0.1 all-gather.5.cloned.1.call-start
  10.7 213.3 %all-gather.3.cloned.1.call-done = bf16[5120,2048]{1,0:T(8,128)(2,1)} async-done(((bf16[640,2048]{1,0:T(8,128)(2,1)}), bf16[5120,2048]{1,0:T(8,128)(2,1)}) %all-gather.3.cloned.1.call-update) | async-done | bytes 20971536 | tf_op jit(solution)/shard_map/all_gather | solution.py:111
  224.0 0.8 collective-permute-start
  224.9 0.0 slice-done.1
  224.9 0.0 slice-done.3
  224.9 1.2 pad_maximum_fusion.1
  226.1 0.1 all-gather.5.cloned.1.call-update
  226.2 0.1 reduce-scatter.3.cloned.1.call-start
  226.3 0.5 copy-done
  226.8 0.8 copy.10
  227.7 1.9 copy.9
  229.5 2.6 copy.11
  232.1 2.7 pad.23.refs_3_
  234.8 2.0 fusion.5.refs_2_
  236.8 0.0 copy-done.1
  236.8 1.0 copy-done.2
  237.8 1.8 fusion.4.refs_4_
  239.5 16.5 %collective-permute-done.refs_0_.refs_1_ = bf16[8,2,320,2048]{3,2,1,0:T(8,128)(2,1)} collective-permute-done((bf16[8,2,320,2048]{3,2,1,0:T(8,128)(2,1)}, bf16[8,2,320,2048]{3,2,1,0:T(8,128)(2,1)}, u32[]{:S(2)}, u32[]{:S(2)}) %collective-permute-start) | collective-permute-done | bytes 20971552 | tf_op jit(solution)/shard_map/ppermute | solution.py:118
  256.0 32.8 %token_part.4 = (bf16[2560,384]{1,0:T(8,128)(2,1)}, bf16[2560,768]{1,0:T(8,128)(2,1)}, bf16[2560,2048]{1,0:T(8,128)(2,1)}) custom-call(bf16[8,2,320,2048]{3,2,1,0:T(8,128)(2,1)} %collective-permute-done.refs_0_.refs_1_, bf16[8,2,320,2048]{3,2,1,0:T(8,128)(2,1)} %collective-permute-done.refs_0_.refs_1_, bf16[2048,768]{1,0:T(8,128)(2,1)} %fusion.5.refs_2_, ...), custom_call_target="tpu_custom_call" | custom-call | flops 20132659200 | bytes 41943040 | tf_op jit(solution)/shard_map/token_part/pallas_call | solution.py:49
  288.8 0.3 collective-permute-start.1
  289.1 65.8 %all-gather.5.cloned.1.call-done = bf16[3072,2048]{1,0:T(8,128)(2,1)} async-done(((bf16[384,2048]{1,0:T(8,128)(2,1)}), bf16[3072,2048]{1,0:T(8,128)(2,1)}) %all-gather.5.cloned.1.call-update) | async-done | bytes 12582928 | tf_op jit(solution)/shard_map/all_gather | solution.py:111
  354.9 0.8 collective-permute-start.2
  355.8 0.0 collective-permute-done.1.refs_5_
  355.8 33.5 %token_part.5 = (bf16[2560,384]{1,0:T(8,128)(2,1)}, bf16[2560,768]{1,0:T(8,128)(2,1)}, bf16[2560,2048]{1,0:T(8,128)(2,1)}) custom-call(bf16[8,2,320,2048]{3,2,1,0:T(8,128)(2,1)} %bitcast.8, bf16[8,2,320,2048]{3,2,1,0:T(8,128)(2,1)} %bitcast.9, bf16[2048,768]{1,0:T(8,128)(2,1)} %fusion.5.refs_2_, bf16[2048,384]{1,0:T(8,128)(2,1)} %pad.23.refs_3_, ...), custom_call_target="tpu_custom_call" | custom-call | flops 20132659200 | bytes 41943040 | tf_op jit(solution)/shard_map/token_part/pallas_call | solution.py:49
  389.3 0.1 reduce-scatter.3.cloned.1.call-update
  389.3 0.1 reduce-scatter.5.cloned.1.call-start
  389.4 20.6 %weight_part.4 = (f32[352,2048]{1,0:T(8,128)}, f32[352,2048]{1,0:T(8,128)}, f32[352,2048]{1,0:T(8,128)}) custom-call(bf16[8,2,320,2048]{3,2,1,0:T(8,128)(2,1)} %collective-permute-done.refs_0_.refs_1_, bf16[8,2,320,2048]{3,2,1,0:T(8,128)(2,1)} %collective-permute-done.refs_0_.refs_1_, bf16[2560,384]{1,0:T(8,128)(2,1)} %get-tuple-element.37.refs_2_, ...), custom_call_target="tpu_custom_call" | custom-call | flops 12079595520 | bytes 38273024 | tf_op jit(solution)/shard_map/weight_part/pallas_call | solution.py:87
  410.0 0.0 collective-permute-done.2.refs_0_.refs_1_
  410.1 21.8 %token_part.6 = (bf16[1536,384]{1,0:T(8,128)(2,1)}, bf16[1536,768]{1,0:T(8,128)(2,1)}, bf16[1536,2048]{1,0:T(8,128)(2,1)}) custom-call(bf16[8,2,192,2048]{3,2,1,0:T(8,128)(2,1)} %collective-permute-done.2.refs_0_.refs_1_, bf16[8,2,192,2048]{3,2,1,0:T(8,128)(2,1)} %collective-permute-done.2.refs_0_.refs_1_, bf16[2048,768]{1,0:T(8,128)(2,1)} %fusion.5.refs_2_, ...), custom_call_target="tpu_custom_call" | custom-call | flops 12079595520 | bytes 25165824 | tf_op jit(solution)/shard_map/token_part/pallas_call | solution.py:49
  431.9 0.0 collective-permute-start.3
  431.9 10.5 %collective-permute-done.3.refs_5_ = bf16[1536,2048]{1,0:T(8,128)(2,1)} collective-permute-done((bf16[1536,2048]{1,0:T(8,128)(2,1)}, bf16[1536,2048]{1,0:T(8,128)(2,1)}, u32[]{:S(2)}, u32[]{:S(2)}) %collective-permute-start.3) | collective-permute-done | bytes 6291488 | tf_op jit(solution)/shard_map/ppermute | solution.py:118
  442.4 22.3 %token_part.7 = (bf16[1536,384]{1,0:T(8,128)(2,1)}, bf16[1536,768]{1,0:T(8,128)(2,1)}, bf16[1536,2048]{1,0:T(8,128)(2,1)}) custom-call(bf16[8,2,192,2048]{3,2,1,0:T(8,128)(2,1)} %bitcast.13, bf16[8,2,192,2048]{3,2,1,0:T(8,128)(2,1)} %bitcast.14, bf16[2048,768]{1,0:T(8,128)(2,1)} %fusion.5.refs_2_, bf16[2048,384]{1,0:T(8,128)(2,1)} %pad.23.refs_3_, ...), custom_call_target="tpu_custom_call" | custom-call | flops 12079595520 | bytes 25165824 | tf_op jit(solution)/shard_map/token_part/pallas_call | solution.py:49
  464.7 0.1 reduce-scatter.5.cloned.1.call-update
  464.8 27.6 %weight_part.5 = (f32[352,2048]{1,0:T(8,128)}, f32[352,2048]{1,0:T(8,128)}, f32[352,2048]{1,0:T(8,128)}) custom-call(bf16[8,2,320,2048]{3,2,1,0:T(8,128)(2,1)} %bitcast.10, bf16[8,2,320,2048]{3,2,1,0:T(8,128)(2,1)} %bitcast.11, bf16[2560,384]{1,0:T(8,128)(2,1)} %get-tuple-element.49.refs_2_, bf16[2560,768]{1,0:T(8,128)(2,1)} %get-tuple-element.50.refs_3_, ...), custom_call_target="tpu_custom_call" | custom-call | flops 12079595520 | bytes 38273024 | tf_op jit(solution)/shard_map/weight_part/pallas_call | solution.py:87
  492.4 21.3 %weight_part.6 = (f32[352,2048]{1,0:T(8,128)}, f32[352,2048]{1,0:T(8,128)}, f32[352,2048]{1,0:T(8,128)}) custom-call(bf16[8,2,192,2048]{3,2,1,0:T(8,128)(2,1)} %collective-permute-done.2.refs_0_.refs_1_, bf16[8,2,192,2048]{3,2,1,0:T(8,128)(2,1)} %collective-permute-done.2.refs_0_.refs_1_, bf16[1536,384]{1,0:T(8,128)(2,1)} %get-tuple-element.45.refs_2_, ...), custom_call_target="tpu_custom_call" | custom-call | flops 7247757312 | bytes 29884416 | tf_op jit(solution)/shard_map/weight_part/pallas_call | solution.py:87
  513.7 21.6 %weight_part.7 = (f32[352,2048]{1,0:T(8,128)}, f32[352,2048]{1,0:T(8,128)}, f32[352,2048]{1,0:T(8,128)}) custom-call(bf16[8,2,192,2048]{3,2,1,0:T(8,128)(2,1)} %bitcast.15, bf16[8,2,192,2048]{3,2,1,0:T(8,128)(2,1)} %bitcast.16, bf16[1536,384]{1,0:T(8,128)(2,1)} %get-tuple-element.43.refs_2_, bf16[1536,768]{1,0:T(8,128)(2,1)} %get-tuple-element.44.refs_3_, ...), custom_call_target="tpu_custom_call" | custom-call | flops 7247757312 | bytes 29884416 | tf_op jit(solution)/shard_map/weight_part/pallas_call | solution.py:87
  535.3 1.6 pad.26
  536.9 34.8 %reduce-scatter.5.cloned.1.call-done = bf16[192,2048]{1,0:T(8,128)(2,1)} async-done(((bf16[1536,2048]{1,0:T(8,128)(2,1)}), bf16[192,2048]{1,0:T(8,128)(2,1)}) %reduce-scatter.5.cloned.1.call-update) | async-done | bytes 786448 | tf_op jit(solution)/shard_map/reduce_scatter | solution.py:115
  571.7 1.2 constant_dynamic-update-slice_fusion
  572.8 0.0 copy-start.3
  572.9 1.3 copy-done.3
  (6 shorter events, 0.0 us)
Async XLA Ops:
  7.2 1.3 slice-start
  7.2 1.7 slice-start.2
  7.2 216.8 %all-gather.3.cloned.1.call-start = ((), (), s32[]{:S(2)}) async-start(), calls=%async_computation.2 | async-start | bytes 23592960 | tf_op jit(solution)/shard_map/all_gather | solution.py:111
  10.6 214.3 %slice-start.1 = ((bf16[512,2048]{1,0:T(8,128)(2,1)}), bf16[192,2048]{1,0:T(8,128)(2,1)S(1)}, s32[]{:S(2)}) async-start(bf16[512,2048]{1,0:T(8,128)(2,1)} %param.5), calls=%async_computation.7 | async-start | bytes 1572864 | tf_op jit(solution)/shard_map/slice | solution.py:130
  10.6 214.3 %slice-start.3 = ((bf16[512,2048]{1,0:T(8,128)(2,1)}), bf16[192,2048]{1,0:T(8,128)(2,1)S(1)}, s32[]{:S(2)}) async-start(bf16[512,2048]{1,0:T(8,128)(2,1)} %param.6), calls=%async_computation.9 | async-start | bytes 1572864 | tf_op jit(solution)/shard_map/slice | solution.py:130
  10.6 344.3 %all-gather.5.cloned.1.call-start = ((), (), s32[]{:S(2)}) async-start(), calls=%async_computation.4 | async-start | bytes 14155776 | tf_op jit(solution)/shard_map/all_gather | solution.py:111
  224.0 32.0 %collective-permute-start = (bf16[8,2,320,2048]{3,2,1,0:T(8,128)(2,1)}, bf16[8,2,320,2048]{3,2,1,0:T(8,128)(2,1)}, u32[]{:S(2)}, u32[]{:S(2)}) collective-permute-start(bf16[8,2,320,2048]{3,2,1,0:T(8,128)(2,1)} %bitcast.7), channel_id=1, source_target_pairs={{0,1},{1,0},{2,3},{3,2},{4,5},{5,4},{6,7},{7,6},{8,9},{9,8},{10,11... | collective-permute-start | bytes 62914568 | tf_op jit(solution)/shard_map/ppermute | solution.py:118
  224.9 1.9 copy-start
  226.2 309.1 %reduce-scatter.3.cloned.1.call-start = ((), (), s32[]{:S(2)}) async-start(), calls=%async_computation.3 | async-start | bytes 11796480 | tf_op jit(solution)/shard_map/reduce_scatter | solution.py:115
  234.8 2.0 copy-start.1
  234.8 2.9 copy-start.2
  288.8 67.0 %collective-permute-start.1 = (bf16[2560,2048]{1,0:T(8,128)(2,1)}, bf16[2560,2048]{1,0:T(8,128)(2,1)}, u32[]{:S(2)}, u32[]{:S(2)}) collective-permute-start(bf16[2560,2048]{1,0:T(8,128)(2,1)} %get-tuple-element.33), channel_id=1, source_target_pairs={{0,1},{1,0},{2,3},{3,2},{4,5},{5,4},{6,7},{7,6},{8,9},{9,8},{10,11... | collective-permute-start | bytes 31457288 | tf_op jit(solution)/shard_map/ppermute | solution.py:118
  354.9 55.1 %collective-permute-start.2 = (bf16[8,2,192,2048]{3,2,1,0:T(8,128)(2,1)}, bf16[8,2,192,2048]{3,2,1,0:T(8,128)(2,1)}, u32[]{:S(2)}, u32[]{:S(2)}) collective-permute-start(bf16[8,2,192,2048]{3,2,1,0:T(8,128)(2,1)} %bitcast.12), channel_id=1, source_target_pairs={{0,1},{1,0},{2,3},{3,2},{4,5},{5,4},{6,7},{7,6},{8,9},{9,8},{10,11... | collective-permute-start | bytes 37748744 | tf_op jit(solution)/shard_map/ppermute | solution.py:118
  389.3 182.3 %reduce-scatter.5.cloned.1.call-start = ((), (), s32[]{:S(2)}) async-start(), calls=%async_computation.5 | async-start | bytes 7077888 | tf_op jit(solution)/shard_map/reduce_scatter | solution.py:115
  431.9 10.5 %collective-permute-start.3 = (bf16[1536,2048]{1,0:T(8,128)(2,1)}, bf16[1536,2048]{1,0:T(8,128)(2,1)}, u32[]{:S(2)}, u32[]{:S(2)}) collective-permute-start(bf16[1536,2048]{1,0:T(8,128)(2,1)} %get-tuple-element.41), channel_id=1, source_target_pairs={{0,1},{1,0},{2,3},{3,2},{4,5},{5,4},{6,7},{7,6},{8,9},{9,8},{10,11... | collective-permute-start | bytes 18874376 | tf_op jit(solution)/shard_map/ppermute | solution.py:118
  572.8 1.3 copy-start.3
Sparse Core Ops, SparseCore 0:
  10.8 213.2 all-gather.2
  226.3 128.5 all-gather.4
  389.5 109.4 reduce-scatter.2
  501.2 70.4 reduce-scatter.4
